TPU v7x, 32 devices: a 4x4x1 block of a 4x4x8 slice. The times are simulated.
32 devices in a mesh: rep: 1 (over z), emb: 4 (over y), model: 8 (over x, core).
Axes of the slice: x: 4, y: 4, z: 1, core: 2. Of those that a mesh axis runs over, the one named last changes fastest.
The devices are a block of a 4x4x8 slice.
Arguments:
- x: bfloat16 [512, 4096], P('rep')
- Wq: bfloat16 [4096, 4096], P('emb', 'model')
- Wk: bfloat16 [4096, 256], replicated
- Wv: bfloat16 [4096, 256], replicated
- Wo: bfloat16 [4096, 4096], P('model', 'emb')
- Kc: bfloat16 [512, 512, 256], P('rep')
- Vc: bfloat16 [512, 512, 256], P('rep')
- lengths: int32 [512], P('rep')
Outputs:
- output 1: bfloat16 [512, 4096], P('rep')
- output 2: bfloat16 [512, 256], P('rep')
- output 3: bfloat16 [512, 256], P('rep')
All inputs are finite; a program needn't handle non-finite values.
Results may differ from a plain program's by a relative error of at most 0.0128483.
Values are sent between devices in bfloat16 or wider.
A program may use at most 768 MiB of HBM per device.

v0:
```python
import jax
import jax.numpy as jnp
from jax import lax
from jax.sharding import PartitionSpec as P


def _attend(q, K, V, kn, vn, lens):
    dh = q.shape[-1]
    t = K.shape[1]
    scale = dh ** -0.5
    s = jnp.einsum('bhd,btd->bht', q, K, preferred_element_type=jnp.float32) * scale
    valid = jnp.arange(t)[None, :] < lens[:, None]
    s = jnp.where(valid[:, None, :], s, -jnp.inf)
    sn = jnp.einsum('bhd,bd->bh', q, kn, preferred_element_type=jnp.float32) * scale
    m = jnp.maximum(jnp.max(s, axis=-1), sn)
    p = jnp.exp(s - m[..., None])
    pn = jnp.exp(sn - m)
    l = jnp.sum(p, axis=-1) + pn
    acc = jnp.einsum('bht,btd->bhd', p.astype(jnp.bfloat16), V, preferred_element_type=jnp.float32)
    acc = acc + pn.astype(jnp.bfloat16).astype(jnp.float32)[..., None] * vn.astype(jnp.float32)[:, None, :]
    return (acc / l[..., None]).astype(jnp.bfloat16)


def solution(mesh):
    ne = mesh.shape['emb']
    nm = mesh.shape['model']

    def local(x, Wq, Wk, Wv, Wo, Kc, Vc, lengths):
        b, d = x.shape
        de = Wq.shape[0]
        dh = Wk.shape[1]
        hl = Wq.shape[1] // dh
        be = b // ne
        bl = be // nm
        i = lax.axis_index('emb')
        j = lax.axis_index('model')
        xi = lax.dynamic_slice_in_dim(x, i * de, de, axis=1)
        qp = jnp.dot(xi, Wq, preferred_element_type=jnp.float32)
        q = lax.psum_scatter(qp, 'emb', scatter_dimension=0, tiled=True)
        q = q.astype(jnp.bfloat16).reshape(be, hl, dh)
        q = lax.all_to_all(q, 'model', 0, 1, tiled=True)
        k_new = jnp.dot(x, Wk, preferred_element_type=jnp.float32).astype(jnp.bfloat16)
        v_new = jnp.dot(x, Wv, preferred_element_type=jnp.float32).astype(jnp.bfloat16)
        start = i * be + j * bl
        K = lax.dynamic_slice_in_dim(Kc, start, bl, 0)
        V = lax.dynamic_slice_in_dim(Vc, start, bl, 0)
        kn = lax.dynamic_slice_in_dim(k_new, start, bl, 0)
        vn = lax.dynamic_slice_in_dim(v_new, start, bl, 0)
        lens = lax.dynamic_slice_in_dim(lengths, start, bl, 0)
        o = _attend(q, K, V, kn, vn, lens)
        o = lax.all_to_all(o, 'model', 1, 0, tiled=True)
        o = lax.all_gather(o, 'emb', axis=0, tiled=True)
        yp = jnp.dot(o.reshape(b, hl * dh), Wo, preferred_element_type=jnp.float32).astype(jnp.bfloat16)
        ys = lax.psum(yp, 'model')
        yi = (xi.astype(jnp.float32) + ys.astype(jnp.float32)).astype(jnp.bfloat16)
        y = lax.all_gather(yi, 'emb', axis=1, tiled=True)
        return y, k_new, v_new

    in_specs = (P('rep', None), P('emb', 'model'), P(), P(), P('model', 'emb'),
                P('rep', None, None), P('rep', None, None), P('rep'))
    out_specs = (P('rep', None), P('rep', None), P('rep', None))
    return jax.shard_map(local, mesh=mesh, in_specs=in_specs, out_specs=out_specs, check_vma=False)
```

profile of v0, /device:TPU:97, one launch (start us, length us, event | category | flops | bytes accessed | tf_op | source)
XLA Modules:
  0.0 194.5 jit_solution(2347222337995526764)
XLA Ops:
  7.2 0.0 copy-start
  7.2 0.1 reduce-scatter.2.cloned.1.call-start
  7.3 3.4 %fusion.19 = f32[512,512]{1,0:T(8,128)} fusion(bf16[1024,512]{1,0:T(8,128)(2,1)} %param.9, bf16[512,4096]{1,0:T(8,128)(2,1)} %param.8, s32[]{:T(128)S(6)} %select_n.14), kind=kOutput, calls=%fused_computation.13 | convolution fusion | flops 536870912 | bytes 3145732 | tf_op jit(solution)/shard_map/dot_general | solution.py:38
  10.6 0.1 reduce-scatter.2.cloned.1.call-update
  10.7 0.9 dynamic_slice.19
  11.6 0.1 iota_compare_fusion
  11.7 3.9 %convolution_convert_fusion.2 = bf16[512,256]{1,0:T(8,128)(2,1)S(1)} fusion(bf16[512,4096]{1,0:T(8,128)(2,1)} %param.8, bf16[4096,256]{1,0:T(8,128)(2,1)S(1)} %copy-done), kind=kOutput, calls=%fused_computation.9 | convolution fusion | flops 1073872896 | bytes 6553600 | tf_op jit(solution)/shard_map/dot_general | solution.py:42
  15.7 0.0 copy-start.3
  15.7 1.3 convolution_convert_fusion.1
  17.0 0.0 copy-start.2
  17.0 17.4 %reduce-scatter.2.cloned.1.call-done = f32[128,512]{1,0:T(8,128)} async-done(((f32[512,512]{1,0:T(8,128)}), f32[128,512]{1,0:T(8,128)}) %reduce-scatter.2.cloned.1.call-update) | async-done | bytes 262160 | tf_op jit(solution)/shard_map/reduce_scatter | solution.py:39
  34.3 1.0 convert_element_type.37
  35.3 0.7 reshape.33
  36.0 6.8 %all-to-all-start = ((bf16[128,2,256]{2,1,0:T(2,128)(2,1)}), bf16[128,2,256]{2,1,0:T(2,128)(2,1)S(1)}, u32[]{:S(2)}, u32[]{:S(2)}) async-start(bf16[128,2,256]{2,1,0:T(2,128)(2,1)} %reshape.33), calls=%async_computation.1 | async-start | bytes 262144 | tf_op jit(solution)/shard_map/all_to_all | solution.py:41
  42.8 5.0 %all-to-all-done = bf16[128,2,256]{2,1,0:T(2,128)(2,1)S(1)} async-done(((bf16[128,2,256]{2,1,0:T(2,128)(2,1)}), bf16[128,2,256]{2,1,0:T(2,128)(2,1)S(1)}, u32[]{:S(2)}, u32[]{:S(2)}) %all-to-all-start) | async-done | bytes 131104 | tf_op jit(solution)/shard_map/all_to_all | solution.py:41
  47.8 0.1 copy.29
  47.9 0.1 all_to_all.29
  48.0 0.1 fusion.25
  48.1 3.5 %fusion.31 = (f32[16,16]{1,0:T(8,128)S(1)}, f32[16,16,512]{2,1,0:T(8,128)S(1)}) fusion(bf16[16,16,256]{2,1,0:T(8,128)(2,1)S(1)} %all_to_all.29, bf16[512,512,256]{2,1,0:T(8,128)(2,1)} %param.13, s32[]{:T(128)S(6)} %select_n.15, pred[16,512]{1,0:T(8,128)(4,1)S(1)} %iota_compare_fusion), kind=kOutput, calls=%fused_computation.32 | convolution fusion | flops 67501824 | bytes 4858884 | tf_op jit(solution)/shard_map/bhd,btd->bht/dot_general | solution.py:11
  51.6 0.2 fusion.21
  51.8 2.9 %fusion.16 = bf16[16,16,256]{2,1,0:T(8,128)(2,1)S(1)} fusion(bf16[512,512,256]{2,1,0:T(8,128)(2,1)} %param.14, s32[]{:T(128)S(6)} %select_n.15, f32[16,16,512]{2,1,0:T(8,128)S(1)} %get-tuple-element.6, f32[16,16]{1,0:T(8,128)S(1)} %multiply_maximum_fusion, f32[16,16]{1,0:T(8,128)S(1)} %get-tuple-element.4, f32[16,256]{1,0:T(8,128)S(1)} %dynamic-slice_convert_fusion, ...), kind=kOutput, calls=%fused_computation.12 | convolution fusion | flops 67633152 | bytes 4869124 | tf_op jit(solution)/shard_map/bht,btd->bhd/dot_general | solution.py:19
  54.8 8.6 %all_to_all.36 = bf16[16,16,256]{2,0,1:T(8,128)(2,1)S(1)} all-to-all(bf16[16,16,256]{2,0,1:T(8,128)(2,1)S(1)} %copy.21), channel_id=1, replica_groups=mesh['rep'=1,'emb'=4,'model'=8] {'model'}, dimensions={1} | all-to-all | bytes 262144 | tf_op jit(solution)/shard_map/all_to_all | solution.py:51
  63.4 9.9 %all_gather.6 = bf16[512,2,256]{2,0,1:T(8,128)(2,1)S(1)} all-gather(bf16[128,2,256]{2,0,1:T(8,128)(2,1)S(1)} %bitcast.22), channel_id=1, replica_groups=mesh['rep'=1,'emb'=4,'model'=8] {'emb'}, dimensions={0}, use_global_device_ids=true | all-gather | bytes 655360 | tf_op jit(solution)/shard_map/all_gather | solution.py:52
  73.3 0.2 copy.23
  73.6 2.9 %convolution_convert_fusion = bf16[512,1024]{1,0:T(8,128)(2,1)} fusion(bf16[512,512]{0,1:T(8,128)(2,1)S(1)} %bitcast.23, bf16[512,1024]{1,0:T(8,128)(2,1)} %param.12), kind=kOutput, calls=%fused_computation.5 | convolution fusion | flops 537395200 | bytes 2621440 | tf_op jit(solution)/shard_map/dot_general | solution.py:53
  76.5 0.1 all-reduce.2.cloned.1.call-update
  76.5 0.1 all-gather.2.cloned.1.call-start
  76.6 56.8 %all-reduce.2.cloned.1.call-done = bf16[512,1024]{1,0:T(8,128)(2,1)} async-done(((bf16[512,1024]{1,0:T(8,128)(2,1)}), bf16[512,1024]{1,0:T(8,128)(2,1)}) %all-reduce.2.cloned.1.call-update) | async-done | bytes 1048592 | tf_op jit(solution)/shard_map/psum | solution.py:54
  133.5 2.9 %add_convert_fusion = bf16[512,1024]{1,0:T(8,128)(2,1)} fusion(bf16[512,1024]{1,0:T(8,128)(2,1)} %all-reduce.2.cloned.1.call-done, bf16[512,4096]{1,0:T(8,128)(2,1)} %param.8, s32[]{:T(128)S(6)} %select_n.14), kind=kLoop, calls=%fused_computation.4 | loop fusion | flops 2097152 | bytes 3145732 | tf_op jit(solution)/shard_map/convert_element_type | solution.py:55
  136.4 0.1 all-gather.2.cloned.1.call-update
  136.4 46.8 %all-gather.2.cloned.1.call-done = bf16[512,4096]{1,0:T(8,128)(2,1)} async-done(((bf16[512,1024]{1,0:T(8,128)(2,1)}), bf16[512,4096]{1,0:T(8,128)(2,1)}) %all-gather.2.cloned.1.call-update) | async-done | bytes 4194320 | tf_op jit(solution)/shard_map/all_gather | solution.py:56
  183.2 4.7 %copy.32 = bf16[512,4096]{1,0:T(8,128)(2,1)} copy(bf16[512,4096]{1,0:T(8,128)(2,1)} %all-gather.2.cloned.1.call-done) | data formatting | bytes 8388608
  (14 shorter events, 0.1 us)
Async XLA Ops:
  7.2 4.5 %copy-start = (bf16[4096,256]{1,0:T(8,128)(2,1)S(1)}, bf16[4096,256]{1,0:T(8,128)(2,1)}, u32[]{:S(2)}) copy-start(bf16[4096,256]{1,0:T(8,128)(2,1)} %param.10) | copy-start | bytes 6291460
  7.2 27.1 %reduce-scatter.2.cloned.1.call-start = ((), (), s32[]{:S(2)}) async-start(), calls=%async_computation.3 | async-start | bytes 1310720 | tf_op jit(solution)/shard_map/reduce_scatter | solution.py:39
  10.7 5.0 %copy-start.1 = (bf16[512,4096]{1,0:T(8,128)(2,1)S(1)}, bf16[512,4096]{1,0:T(8,128)(2,1)}, u32[]{:S(2)}) copy-start(bf16[512,4096]{1,0:T(8,128)(2,1)} %param.8) | copy-start | bytes 12582916
  10.7 5.0 %copy-start.4 = (bf16[4096,256]{1,0:T(8,128)(2,1)S(1)}, bf16[4096,256]{1,0:T(8,128)(2,1)}, u32[]{:S(2)}) copy-start(bf16[4096,256]{1,0:T(8,128)(2,1)} %param.11) | copy-start | bytes 6291460
  15.7 27.1 %copy-start.3 = (bf16[512,256]{1,0:T(8,128)(2,1)}, bf16[512,256]{1,0:T(8,128)(2,1)S(1)}, u32[]{:S(2)}) copy-start(bf16[512,256]{1,0:T(8,128)(2,1)S(1)} %convolution_convert_fusion.2) | copy-start | bytes 786436
  17.0 37.8 %copy-start.2 = (bf16[512,256]{1,0:T(8,128)(2,1)}, bf16[512,256]{1,0:T(8,128)(2,1)S(1)}, u32[]{:S(2)}) copy-start(bf16[512,256]{1,0:T(8,128)(2,1)S(1)} %convolution_convert_fusion.1) | copy-start | bytes 786436
  36.0 11.8 %all-to-all-start = ((bf16[128,2,256]{2,1,0:T(2,128)(2,1)}), bf16[128,2,256]{2,1,0:T(2,128)(2,1)S(1)}, u32[]{:S(2)}, u32[]{:S(2)}) async-start(bf16[128,2,256]{2,1,0:T(2,128)(2,1)} %reshape.33), calls=%async_computation.1 | async-start | bytes 262144 | tf_op jit(solution)/shard_map/all_to_all | solution.py:41
  42.8 90.7 %all-reduce.2.cloned.1.call-start = ((), (), s32[]{:S(2)}) async-start(), calls=%async_computation.4 | async-start | bytes 2097152 | tf_op jit(solution)/shard_map/psum | solution.py:54
  76.5 106.7 %all-gather.2.cloned.1.call-start = ((), (), s32[]{:S(2)}) async-start(), calls=%async_computation.5 | async-start | bytes 5242880 | tf_op jit(solution)/shard_map/all_gather | solution.py:56
Sparse Core Ops, SparseCore 0:
  10.9 23.3 reduce-scatter.1
  76.7 56.7 all-reduce.1
  136.6 46.6 all-gather.1
where the time goes:
time: 195 us; the launch traced here: 194 us
  waiting for transfers between devices  126 us (65%)
  blocking collectives  18.5 us (9%)
  matrix products  18 us (9%)
  between operations  13.9 us (7%)
  starting transfers between devices  6.9 us (4%)
  local copies, waits for them, and re-layouts  6.76 us (3%)
  other arithmetic  4.23 us (2%)
    psum x1, waiting for transfers between devices, local(): ys = lax.psum(yp, 'model')  56.8 us
    all_gather x1, waiting for transfers between devices, local(): y = lax.all_gather(yi, 'emb', axis=1, tiled=True)  46.8 us
    reduce_scatter x1, waiting for transfers between devices, local(): q = lax.psum_scatter(qp, 'emb', scatter_dimension=0, tiled=True)  17.4 us
    all_gather x1, blocking collectives, local(): o = lax.all_gather(o, 'emb', axis=0, tiled=True)  9.95 us
    all_to_all x1, blocking collectives, local(): o = lax.all_to_all(o, 'model', 1, 0, tiled=True)  8.57 us
    all_to_all x1, starting transfers between devices, local(): q = lax.all_to_all(q, 'model', 0, 1, tiled=True)  6.77 us
    all_to_all x1, waiting for transfers between devices, local(): q = lax.all_to_all(q, 'model', 0, 1, tiled=True)  4.99 us
    unnamed x11, local copies, waits for them, and re-layouts  4.73 us
  transfers between devices with their start and end apart: 4, of which 4 were waited for; matrix products, arithmetic and copies ran while one was open for 3% of the time, Pallas kernels for 0%

commit v1 on v0

v1 whole, which is shorter than its diff:
```python
import functools

import jax
import jax.numpy as jnp
from jax import lax
from jax.experimental import pallas as pl
from jax.experimental.pallas import tpu as pltpu
from jax.sharding import PartitionSpec as P

CORES = 2
LANES = 128
F32 = jnp.float32
BF16 = jnp.bfloat16


def _mod(a, n):
    return lax.rem(a + 2 * n, n)


def _kernel(ne, nm, H, lens_ref, x_hbm, wq_hbm, wk_hbm, wv_hbm, wo_hbm, kc_hbm, vc_hbm,
            y_ref, kn_ref, vn_ref,
            xv, wq_v, wkv, k_v, v_v, wo_v, s_opp, s_up, s_dn, s_own, rel_p, rel_m, fin_p, fin_m,
            qb, qr, q32, kv32, o32, o_all,
            lsem, q_ss, q_rs, a_ss, a_rs, w_ss, w_rs, d_ss, d_rs, o_ss, o_rs, y_ss, y_rs, c_ss, c_rs):
    nx = nm // CORES
    i = lax.axis_index('emb')
    j = lax.axis_index('model')
    X = lax.div(j, CORES)
    c = lax.rem(j, CORES)
    de = xv.shape[2]
    be = s_opp.shape[0]
    bl = qr.shape[1]
    nl = q32.shape[0]
    dh = nl * LANES
    hl = H // nm
    nw = wo_v.shape[2]
    hb = be // 2
    start = pl.multiple_of(i * be + j * bl, bl)
    T = k_v.shape[1]
    scale = dh ** -0.5

    def dev(yy, xx, cc):
        return {'emb': yy, 'model': xx * CORES + cc}

    def row(jj):
        return {'emb': i, 'model': jj}

    def rcopy(src, dst, ss, rs, to):
        return pltpu.make_async_remote_copy(src_ref=src, dst_ref=dst, send_sem=ss, recv_sem=rs,
                                            device_id=to, device_id_type=pl.DeviceIdType.MESH)

    up, dn, opp = _mod(i + 1, ne), _mod(i - 1, ne), _mod(i + 2, ne)
    partner = dev(i, X, 1 - c)

    barrier = pltpu.get_barrier_semaphore()
    for k in range(1, nm):
        pl.semaphore_signal(barrier, inc=1, device_id=row(_mod(j + k, nm)), device_id_type=pl.DeviceIdType.MESH)
    for yy in (up, dn):
        pl.semaphore_signal(barrier, inc=1, device_id={'emb': yy, 'model': j}, device_id_type=pl.DeviceIdType.MESH)

    def load(n, src, dst):
        cp = pltpu.make_async_copy(src, dst, lsem.at[n])
        cp.start()
        return cp

    def xblock(n, blk):
        return load(n, x_hbm.at[:, pl.ds(pl.multiple_of(blk * de, de), de)], xv.at[blk])

    ld_x = [xblock(0, i)]
    ld_wq = load(4, wq_hbm, wq_v)
    ld_x += [xblock(k, _mod(i + k, ne)) for k in range(1, ne)]
    ld_wk = load(5, wk_hbm, wkv.at[:, pl.ds(0, dh)])
    ld_wv = load(6, wv_hbm, wkv.at[:, pl.ds(dh, dh)])
    ld_k = load(7, kc_hbm.at[pl.ds(start, bl)], k_v)
    ld_v = load(8, vc_hbm.at[pl.ds(start, bl)], v_v)
    ld_wo = load(9, wo_hbm.at[:, pl.ds(pl.multiple_of(X * nw, nw), nw)], wo_v.at[j])

    pl.semaphore_wait(barrier, nm - 1 + 2)

    sends = []

    def go(cp):
        cp.start()
        sends.append(cp)

    for k in (1, nx - 1, *range(2, nx - 1)):
        t = _mod(X + k, nx)
        go(rcopy(wo_hbm.at[:, pl.ds(pl.multiple_of(t * nw, nw), nw)], wo_v.at[j], w_ss.at[k], w_rs.at[k],
                 dev(i, t, c)))

    ld_x[0].wait()
    ld_wq.wait()

    def part(d, buf):
        buf[...] = jnp.dot(xv[i, pl.ds(pl.multiple_of(d * be, be), be), :], wq_v[...], preferred_element_type=F32)

    lo, hi = pl.ds(0, hb), pl.ds(hb, hb)
    to_up, to_dn = {'emb': up, 'model': j}, {'emb': dn, 'model': j}
    part(opp, s_opp)
    go(rcopy(s_opp.at[lo], rel_p, q_ss.at[0], q_rs.at[0], to_up))
    go(rcopy(s_opp.at[hi], rel_m, q_ss.at[1], q_rs.at[1], to_dn))
    part(up, s_up)
    go(rcopy(s_up.at[hi], fin_p.at[hi], q_ss.at[2], q_rs.at[2], to_up))
    part(dn, s_dn)
    go(rcopy(s_dn.at[lo], fin_m.at[lo], q_ss.at[3], q_rs.at[3], to_dn))
    part(i, s_own)

    for ld in ld_x[1:]:
        ld.wait()
    ld_wk.wait()
    ld_wv.wait()

    rows_m = kn_ref.shape[0] // ne

    def kv_rows(m, _):
        rows = pl.ds(pl.multiple_of(m * rows_m, rows_m), rows_m)
        acc = jnp.dot(xv[0, rows, :], wkv[0:de, :], preferred_element_type=F32)
        for blk in range(1, ne):
            acc = acc + jnp.dot(xv[blk, rows, :], wkv[blk * de:(blk + 1) * de, :], preferred_element_type=F32)
        kn_ref[rows, :] = acc[:, :dh].astype(BF16)
        vn_ref[rows, :] = acc[:, dh:].astype(BF16)
        return 0

    lax.fori_loop(0, ne, kv_rows, 0)

    rcopy(rel_p, rel_p, q_ss.at[0], q_rs.at[0], to_up).wait_recv()
    s_up[0:hb, :] = s_up[0:hb, :] + rel_p[...]
    go(rcopy(s_up.at[lo], fin_p.at[lo], q_ss.at[4], q_rs.at[4], to_up))
    rcopy(rel_m, rel_m, q_ss.at[1], q_rs.at[1], to_dn).wait_recv()
    s_dn[hb:be, :] = s_dn[hb:be, :] + rel_m[...]
    go(rcopy(s_dn.at[hi], fin_m.at[hi], q_ss.at[5], q_rs.at[5], to_dn))

    rcopy(fin_p.at[hi], fin_p.at[hi], q_ss.at[2], q_rs.at[2], to_up).wait_recv()
    rcopy(fin_m.at[lo], fin_m.at[lo], q_ss.at[3], q_rs.at[3], to_dn).wait_recv()
    rcopy(fin_p.at[lo], fin_p.at[lo], q_ss.at[4], q_rs.at[4], to_up).wait_recv()
    rcopy(fin_m.at[hi], fin_m.at[hi], q_ss.at[5], q_rs.at[5], to_dn).wait_recv()
    qb[...] = (s_own[...] + fin_p[...] + fin_m[...]).astype(BF16).reshape(qb.shape)
    for k in range(1, nm):
        t = _mod(j + k, nm)
        go(rcopy(qb.at[t], qr.at[j], a_ss.at[k], a_rs.at[k], row(t)))
    qr[j] = qb[j]

    ld_wo.wait()
    go(rcopy(wo_v.at[j], wo_v.at[j], d_ss.at[0], d_rs.at[0], partner))
    for k in range(1, nx):
        src = _mod(X - k, nx) * CORES + c
        rcopy(wo_v.at[src], wo_v.at[src], w_ss.at[k], w_rs.at[k], partner).wait_recv()
        go(rcopy(wo_v.at[src], wo_v.at[src], d_ss.at[k], d_rs.at[k], partner))

    kv32[0] = kn_ref[pl.ds(start, bl), :].astype(F32)
    kv32[1] = vn_ref[pl.ds(start, bl), :].astype(F32)
    ld_k.wait()
    ld_v.wait()

    for k in range(1, nm):
        src = _mod(j - k, nm)
        rcopy(qr.at[src], qr.at[src], a_ss.at[k], a_rs.at[k], partner).wait_recv()
    for jj in range(nm):
        for h in range(hl):
            for n in range(nl):
                q32[n, (jj * hl + h) * bl:(jj * hl + h + 1) * bl, :] = (
                    qr[jj, :, h * dh + n * LANES:h * dh + (n + 1) * LANES].astype(F32))

    def attend(b, _):
        q = jnp.concatenate([q32[n, pl.ds(b, H, stride=bl), :] for n in range(nl)], axis=1)
        s = lax.dot_general(q.astype(BF16), k_v[b], (((1,), (1,)), ((), ())), preferred_element_type=F32) * scale
        n = lens_ref[start + b]
        s = jnp.where(lax.broadcasted_iota(jnp.int32, (H, T), 1) < n, s, -jnp.inf)
        sn = jnp.sum(q * kv32[0, pl.ds(b, 1), :], axis=1, keepdims=True) * scale
        m = jnp.maximum(jnp.max(s, axis=1, keepdims=True), sn)
        p = jnp.exp(s - m)
        pn = jnp.exp(sn - m)
        l = jnp.sum(p, axis=1, keepdims=True) + pn
        acc = jnp.dot(p.astype(BF16), v_v[b], preferred_element_type=F32)
        acc = acc + pn.astype(BF16).astype(F32) * kv32[1, pl.ds(b, 1), :]
        o = acc / l
        for n in range(nl):
            o32[n, pl.ds(b, H, stride=bl), :] = o[:, n * LANES:(n + 1) * LANES]
        return 0

    lax.fori_loop(0, bl, attend, 0, unroll=4)

    chip = i * nx + X
    for h in range(H):
        for n in range(nl):
            o_all[h, chip, :, n * LANES:(n + 1) * LANES] = o32[n, h * bl:(h + 1) * bl, :].astype(BF16)

    def gather(piece, ss, rs, arrived):
        class Half:
            def __init__(self, n):
                self.base, self.q = n * 20, 2 * n
                self.x_first = n == 0

            def piece(self, dp, ds, q, n):
                if self.x_first:
                    return piece(_mod(i + ds, ne), _mod(X + dp, nx), self.q + q, n)
                return piece(_mod(i + dp, ne), _mod(X + ds, nx), self.q + q, n)

            def to(self, dp, ds):
                if self.x_first:
                    return dev(_mod(i + ds, ne), _mod(X + dp, nx), c)
                return dev(_mod(i + dp, ne), _mod(X + ds, nx), c)

            def send(self, mid, ref, to):
                go(rcopy(ref, ref, ss.at[self.base + mid], rs.at[self.base + mid], to))

            def wait(self, mid, ref):
                rcopy(ref, ref, ss.at[self.base + mid], rs.at[self.base + mid], partner).wait_recv()
                arrived(ref)

            def s1(self):
                for d, sg in enumerate((1, -1)):
                    self.send(d, self.piece(0, 0, 0, 2), self.to(sg, 0))

            def w1s2(self):
                for d, sg in enumerate((1, -1)):
                    self.wait(d, self.piece(-sg, 0, 0, 2))
                    self.send(2 + d, self.piece(-sg, 0, d, 1), self.to(sg, 0))

            def w2(self):
                for d, sg in enumerate((1, -1)):
                    self.wait(2 + d, self.piece(2, 0, d, 1))

            def s3(self, k):
                for d, sg in enumerate((1, -1)):
                    self.send(4 + 2 * k + d, self.piece(ITEMS[k], 0, 0, 2), self.to(0, sg))

            def w3s4(self, k):
                for d, sg in enumerate((1, -1)):
                    self.wait(4 + 2 * k + d, self.piece(ITEMS[k], -sg, 0, 2))
                    self.send(12 + 2 * k + d, self.piece(ITEMS[k], -sg, d, 1), self.to(0, sg))

            def w4(self, k):
                for d, sg in enumerate((1, -1)):
                    self.wait(12 + 2 * k + d, self.piece(ITEMS[k], 2, d, 1))

        ITEMS = (0, -1, 1, 2)
        halves = (Half(0), Half(1))

        def both(name, *a):
            for hf in halves:
                getattr(hf, name)(*a)

        both('s1')
        both('s3', 0)
        arrived(piece(i, X, 0, 4))
        both('w1s2')
        both('s3', 1)
        both('s3', 2)
        both('w3s4', 0)
        both('w2')
        both('s3', 3)
        both('w3s4', 1)
        both('w3s4', 2)
        both('w3s4', 3)
        for k in range(4):
            both('w4', k)

    hq = H // 4
    gather(lambda yy, xx, q, n: o_all.at[pl.ds(q * hq, n * hq), yy * nx + xx], o_ss, o_rs, lambda ref: None)

    for k in range(nx):
        src = _mod(X - k, nx) * CORES + (1 - c)
        rcopy(wo_v.at[src], wo_v.at[src], d_ss.at[k], d_rs.at[k], partner).wait_recv()

    rows = ne * nx * bl
    acc = None
    for h in range(H):
        t = jnp.dot(o_all[h].reshape(rows, dh), wo_v[h // hl, (h % hl) * dh:(h % hl + 1) * dh, :],
                    preferred_element_type=F32)
        acc = t if acc is None else acc + t
    cols = pl.ds(pl.multiple_of(chip * nw, nw), nw)
    mine = pl.ds(pl.multiple_of(X * nw, nw), nw)
    for r in range(ne):
        for xx in range(nx):
            g = (r * nx + xx) * bl
            res = xv[i, pl.ds(pl.multiple_of(r * be + (xx * CORES + c) * bl, bl), bl), mine].astype(F32)
            y_ref[r, xx, c, :, cols] = (res + acc[g:g + bl, :].astype(BF16).astype(F32)).astype(BF16)

    def to_partner(ref):
        rcopy(ref, ref, c_ss, c_rs, partner).start()

    gather(lambda yy, xx, q, n: y_ref.at[pl.ds(q, n), :, c, :, pl.ds(pl.multiple_of((yy * nx + xx) * nw, nw), nw)],
           y_ss, y_rs, to_partner)

    other, own = y_ref.at[:, :, 1 - c], y_ref.at[:, :, c]
    rcopy(own, other, c_ss, c_rs, partner).wait_recv()
    rcopy(own, other, c_ss, c_rs, partner).wait_send()
    for cp in sends:
        cp.wait_send()


def solution(mesh):
    ne = mesh.shape['emb']
    nm = mesh.shape['model']

    def local(x, Wq, Wk, Wv, Wo, Kc, Vc, lengths):
        b, d = x.shape
        de = Wq.shape[0]
        dh = Wk.shape[1]
        hl = Wq.shape[1] // dh
        H = hl * nm
        nx = nm // CORES
        be = b // ne
        bl = be // nm
        T = Kc.shape[1]
        nw = Wo.shape[1] // nx
        hd = hl * dh
        V = pltpu.VMEM
        DMA = pltpu.SemaphoreType.DMA
        hbm = pl.BlockSpec(memory_space=pl.ANY)
        vmem = pl.BlockSpec(memory_space=pltpu.VMEM)
        y, kn, vn = pl.pallas_call(
            functools.partial(_kernel, ne, nm, H),
            out_shape=(jax.ShapeDtypeStruct((ne, nx, CORES, bl, d), BF16),
                       jax.ShapeDtypeStruct((b, dh), BF16),
                       jax.ShapeDtypeStruct((b, dh), BF16)),
            in_specs=[pl.BlockSpec(memory_space=pltpu.SMEM)] + [hbm] * 7,
            out_specs=(vmem, vmem, vmem),
            scratch_shapes=[
                V((ne, b, de), BF16), V((de, hd), BF16), V((d, 2 * dh), BF16),
                V((bl, T, dh), BF16), V((bl, T, dh), BF16), V((nm, hd, nw), BF16),
                V((be, hd), F32), V((be, hd), F32), V((be, hd), F32), V((be, hd), F32),
                V((be // 2, hd), F32), V((be // 2, hd), F32), V((be, hd), F32), V((be, hd), F32),
                V((nm, bl, hd), BF16), V((nm, bl, hd), BF16), V((dh // LANES, H * bl, LANES), F32),
                V((2, bl, dh), F32), V((dh // LANES, H * bl, LANES), F32), V((H, ne * nx, bl, dh), BF16),
                DMA((10,)), DMA((6,)), DMA((6,)), DMA((nm,)), DMA((nm,)), DMA((nx,)), DMA((nx,)),
                DMA((nx,)), DMA((nx,)), DMA((40,)), DMA((40,)), DMA((40,)), DMA((40,)), DMA, DMA,
            ],
            compiler_params=pltpu.CompilerParams(collective_id=0, has_side_effects=True,
                                                 vmem_limit_bytes=60 * 1024 * 1024),
        )(lengths, x, Wq, Wk, Wv, Wo, Kc, Vc)
        return y.reshape(b, d), kn, vn

    in_specs = (P('rep', None), P('emb', 'model'), P(), P(), P('model', 'emb'),
                P('rep', None, None), P('rep', None, None), P('rep'))
    out_specs = (P('rep', None), P('rep', None), P('rep', None))
    return jax.shard_map(local, mesh=mesh, in_specs=in_specs, out_specs=out_specs, check_vma=False)
```

time: 195 us -> 73.7 us (0.38)
  waiting for transfers between devices: 126 us -> 0 us
  Pallas kernels: 0 us -> 66.8 us
  blocking collectives: 18.5 us -> 0 us
  matrix products: 18 us -> 0 us
  between operations: 13.9 us -> 0.66 us
  starting transfers between devices: 6.9 us -> 0 us
  other arithmetic: 4.23 us -> 0 us
    pallas_call x0 -> x1, Pallas kernels: none -> 66.8 us  [local(): pl.pallas_call(functools.partial(_kernel, ne, nm, H), out_shape=(jax.Shap...]
    psum x1 -> x0, waiting for transfers between devices: 56.8 us -> none  [local(): ys = lax.psum(yp, 'model')]
    all_gather x1 -> x0, waiting for transfers between devices: 46.8 us -> none  [local(): y = lax.all_gather(yi, 'emb', axis=1, tiled=True)]
    dot_general x7 -> x0, matrix products: 18 us -> none  [the longest x1 3.94 us: local(): jnp.dot(x, Wk, preferred_element_type=jnp.float32).astype(jnp.bfloat16)]
    reduce_scatter x1 -> x0, waiting for transfers between devices: 17.4 us -> none  [local(): q = lax.psum_scatter(qp, 'emb', scatter_dimension=0, tiled=True)]
    all_gather x1 -> x0, blocking collectives: 9.95 us -> none  [local(): o = lax.all_gather(o, 'emb', axis=0, tiled=True)]
    all_to_all x1 -> x0, blocking collectives: 8.57 us -> none  [local(): o = lax.all_to_all(o, 'model', 1, 0, tiled=True)]
    all_to_all x1 -> x0, starting transfers between devices: 6.77 us -> none  [local(): q = lax.all_to_all(q, 'model', 0, 1, tiled=True)]
  transfers between devices with their start and end apart: 4 -> 0, of which waited for: 4 -> 0; matrix products, arithmetic and copies ran while one was open for 3% -> 0% of each run, Pallas kernels for 0% -> 0%
where the time goes in v1:
time: 73.7 us; the launch traced here: 73.6 us
  Pallas kernels  66.8 us (91%)
  local copies, waits for them, and re-layouts  6.17 us (8%)
    pallas_call x1, Pallas kernels, local(): pl.pallas_call(functools.partial(_kernel, ne, nm, H), out_shape=(jax.Shap...  66.8 us
    unnamed x7, local copies, waits for them, and re-layouts  6.17 us

profile of v1, /device:TPU:97, one launch (start us, length us, event | category | flops | bytes accessed | tf_op | source)
XLA Modules:
  0.0 73.6 jit_solution(4433311672552458929)
XLA Ops:
  0.6 66.8 %shard_map.103 = (bf16[4,4,2,16,4096]{4,3,2,1,0:T(8,128)(2,1)}, bf16[512,256]{1,0:T(8,128)(2,1)}, bf16[512,256]{1,0:T(8,128)(2,1)}) custom-call(s32[512]{0:T(512)} %lens_ref.1, bf16[512,4096]{1,0:T(8,128)(2,1)} %x_hbm.1, bf16[1024,512]{1,0:T(8,128)(2,1)} %wq_hbm.1, bf16[4096,256]{1,0:T(8,128)(2,1)} %wk_hbm.1, bf16[4096,256]{1,0:T(8,128)(2,1)} %wv_hbm.1, ...), custom_call_target="tpu_custom_call" | custom-call | tf_op jit(solution)/shard_map/pallas_call | solution.py:313
  67.5 0.0 copy-start.1
  67.5 0.0 copy-start
  67.5 4.8 %copy.14 = bf16[512,4096]{1,0:T(8,128)(2,1)} copy(bf16[512,4096]{1,0:T(8,128)(2,1)} %bitcast.1) | data formatting | bytes 8388608
  72.2 0.0 copy-done.1
  72.2 0.7 copy.15
  72.9 0.0 copy-done
  72.9 0.7 copy.16
Async XLA Ops:
  67.5 4.8 %copy-start.1 = (bf16[512,256]{1,0:T(8,128)(2,1)S(1)}, bf16[512,256]{1,0:T(8,128)(2,1)}, u32[]{:S(2)}) copy-start(bf16[512,256]{1,0:T(8,128)(2,1)} %get-tuple-element.13) | copy-start | bytes 786436
  67.5 5.5 %copy-start = (bf16[512,256]{1,0:T(8,128)(2,1)S(1)}, bf16[512,256]{1,0:T(8,128)(2,1)}, u32[]{:S(2)}) copy-start(bf16[512,256]{1,0:T(8,128)(2,1)} %get-tuple-element.14) | copy-start | bytes 786436

commit v2 on v1

--- a/solution.py
+++ b/solution.py
@@ -20,7 +20,7 @@
 def _kernel(ne, nm, H, lens_ref, x_hbm, wq_hbm, wk_hbm, wv_hbm, wo_hbm, kc_hbm, vc_hbm,
             y_ref, kn_ref, vn_ref,
             xv, wq_v, wkv, k_v, v_v, wo_v, s_opp, s_up, s_dn, s_own, rel_p, rel_m, fin_p, fin_m,
-            qb, qr, q32, kv32, o32, o_all,
+            wo_rel, qb, qr, q32, kv32, o32, o_all,
             lsem, q_ss, q_rs, a_ss, a_rs, w_ss, w_rs, d_ss, d_rs, o_ss, o_rs, y_ss, y_rs, c_ss, c_rs):
     nx = nm // CORES
     i = lax.axis_index('emb')
@@ -33,7 +33,7 @@
     nl = q32.shape[0]
     dh = nl * LANES
     hl = H // nm
-    nw = wo_v.shape[2]
+    hd, nw = wo_v.shape[1:]
     hb = be // 2
     start = pl.multiple_of(i * be + j * bl, bl)
     T = k_v.shape[1]
@@ -75,19 +75,12 @@
     ld_v = load(8, vc_hbm.at[pl.ds(start, bl)], v_v)
     ld_wo = load(9, wo_hbm.at[:, pl.ds(pl.multiple_of(X * nw, nw), nw)], wo_v.at[j])
 
-    pl.semaphore_wait(barrier, nm - 1 + 2)
-
     sends = []
 
     def go(cp):
         cp.start()
         sends.append(cp)
 
-    for k in (1, nx - 1, *range(2, nx - 1)):
-        t = _mod(X + k, nx)
-        go(rcopy(wo_hbm.at[:, pl.ds(pl.multiple_of(t * nw, nw), nw)], wo_v.at[j], w_ss.at[k], w_rs.at[k],
-                 dev(i, t, c)))
-
     ld_x[0].wait()
     ld_wq.wait()
 
@@ -97,8 +90,20 @@
     lo, hi = pl.ds(0, hb), pl.ds(hb, hb)
     to_up, to_dn = {'emb': up, 'model': j}, {'emb': dn, 'model': j}
     part(opp, s_opp)
+    pl.semaphore_wait(barrier, nm - 1 + 2)
     go(rcopy(s_opp.at[lo], rel_p, q_ss.at[0], q_rs.at[0], to_up))
     go(rcopy(s_opp.at[hi], rel_m, q_ss.at[1], q_rs.at[1], to_dn))
+    east, west, far = _mod(X + 1, nx), _mod(X - 1, nx), _mod(X + 2, nx)
+    wo_lo, wo_hi = pl.ds(0, hd // 2), pl.ds(hd // 2, hd // 2)
+
+    def wo_cols(rows, t):
+        return wo_hbm.at[rows, pl.ds(pl.multiple_of(t * nw, nw), nw)]
+
+    go(rcopy(wo_cols(pl.ds(0, hd), east), wo_v.at[j], w_ss.at[0], w_rs.at[0], dev(i, east, c)))
+    go(rcopy(wo_cols(pl.ds(0, hd), west), wo_v.at[j], w_ss.at[1], w_rs.at[1], dev(i, west, c)))
+    go(rcopy(wo_cols(wo_lo, far), wo_rel.at[0], w_ss.at[2], w_rs.at[2], dev(i, east, c)))
+    go(rcopy(wo_cols(wo_hi, far), wo_rel.at[1], w_ss.at[3], w_rs.at[3], dev(i, west, c)))
+
     part(up, s_up)
     go(rcopy(s_up.at[hi], fin_p.at[hi], q_ss.at[2], q_rs.at[2], to_up))
     part(dn, s_dn)
@@ -140,12 +145,23 @@
         go(rcopy(qb.at[t], qr.at[j], a_ss.at[k], a_rs.at[k], row(t)))
     qr[j] = qb[j]
 
+    s_west, s_east, s_far = west * CORES + c, east * CORES + c, far * CORES + c
+    rcopy(wo_rel.at[0], wo_rel.at[0], w_ss.at[2], w_rs.at[2], partner).wait_recv()
+    go(rcopy(wo_rel.at[0], wo_v.at[s_west, wo_lo], w_ss.at[4], w_rs.at[4], dev(i, east, c)))
+    rcopy(wo_rel.at[1], wo_rel.at[1], w_ss.at[3], w_rs.at[3], partner).wait_recv()
+    go(rcopy(wo_rel.at[1], wo_v.at[s_east, wo_hi], w_ss.at[5], w_rs.at[5], dev(i, west, c)))
     ld_wo.wait()
-    go(rcopy(wo_v.at[j], wo_v.at[j], d_ss.at[0], d_rs.at[0], partner))
-    for k in range(1, nx):
-        src = _mod(X - k, nx) * CORES + c
-        rcopy(wo_v.at[src], wo_v.at[src], w_ss.at[k], w_rs.at[k], partner).wait_recv()
-        go(rcopy(wo_v.at[src], wo_v.at[src], d_ss.at[k], d_rs.at[k], partner))
+
+    def to_core(n, ref):
+        go(rcopy(ref, ref, d_ss.at[n], d_rs.at[n], partner))
+
+    def wo_here(n, ref):
+        rcopy(ref, ref, w_ss.at[n], w_rs.at[n], partner).wait_recv()
+        return ref
+
+    to_core(0, wo_v.at[j])
+    to_core(1, wo_here(0, wo_v.at[s_west]))
+    to_core(2, wo_here(1, wo_v.at[s_east]))
 
     kv32[0] = kn_ref[pl.ds(start, bl), :].astype(F32)
     kv32[1] = vn_ref[pl.ds(start, bl), :].astype(F32)
@@ -178,8 +194,11 @@
             o32[n, pl.ds(b, H, stride=bl), :] = o[:, n * LANES:(n + 1) * LANES]
         return 0
 
-    lax.fori_loop(0, bl, attend, 0, unroll=4)
-
+    lax.fori_loop(0, bl, attend, 0, unroll=8)
+
+    wo_here(4, wo_v.at[s_far, wo_lo])
+    wo_here(5, wo_v.at[s_far, wo_hi])
+    to_core(3, wo_v.at[s_far])
     chip = i * nx + X
     for h in range(H):
         for n in range(nl):
@@ -259,9 +278,9 @@
     hq = H // 4
     gather(lambda yy, xx, q, n: o_all.at[pl.ds(q * hq, n * hq), yy * nx + xx], o_ss, o_rs, lambda ref: None)
 
-    for k in range(nx):
-        src = _mod(X - k, nx) * CORES + (1 - c)
-        rcopy(wo_v.at[src], wo_v.at[src], d_ss.at[k], d_rs.at[k], partner).wait_recv()
+    for k, src in enumerate((X, west, east, far)):
+        ref = wo_v.at[src * CORES + 1 - c]
+        rcopy(ref, ref, d_ss.at[k], d_rs.at[k], partner).wait_recv()
 
     rows = ne * nx * bl
     acc = None
@@ -288,6 +307,15 @@
     rcopy(own, other, c_ss, c_rs, partner).wait_send()
     for cp in sends:
         cp.wait_send()
+
+
+def _write_out(y_in, kn_in, vn_in, y_out, kn_out, vn_out, sem):
+    copies = [pltpu.make_async_copy(a, b, sem.at[n])
+              for n, (a, b) in enumerate(((y_in, y_out), (kn_in, kn_out), (vn_in, vn_out)))]
+    for cp in copies:
+        cp.start()
+    for cp in copies:
+        cp.wait()
 
 
 def solution(mesh):
@@ -308,13 +336,11 @@
         hd = hl * dh
         V = pltpu.VMEM
         DMA = pltpu.SemaphoreType.DMA
-        hbm = pl.BlockSpec(memory_space=pl.ANY)
+        hbm = pl.BlockSpec(memory_space=pltpu.HBM)
         vmem = pl.BlockSpec(memory_space=pltpu.VMEM)
-        y, kn, vn = pl.pallas_call(
+        outs = pl.pallas_call(
             functools.partial(_kernel, ne, nm, H),
-            out_shape=(jax.ShapeDtypeStruct((ne, nx, CORES, bl, d), BF16),
-                       jax.ShapeDtypeStruct((b, dh), BF16),
-                       jax.ShapeDtypeStruct((b, dh), BF16)),
+            out_shape=(V((ne, nx, CORES, bl, d), BF16), V((b, dh), BF16), V((b, dh), BF16)),
             in_specs=[pl.BlockSpec(memory_space=pltpu.SMEM)] + [hbm] * 7,
             out_specs=(vmem, vmem, vmem),
             scratch_shapes=[
@@ -322,14 +348,21 @@
                 V((bl, T, dh), BF16), V((bl, T, dh), BF16), V((nm, hd, nw), BF16),
                 V((be, hd), F32), V((be, hd), F32), V((be, hd), F32), V((be, hd), F32),
                 V((be // 2, hd), F32), V((be // 2, hd), F32), V((be, hd), F32), V((be, hd), F32),
-                V((nm, bl, hd), BF16), V((nm, bl, hd), BF16), V((dh // LANES, H * bl, LANES), F32),
+                V((2, hd // 2, nw), BF16), V((nm, bl, hd), BF16), V((nm, bl, hd), BF16), V((dh // LANES, H * bl, LANES), F32),
                 V((2, bl, dh), F32), V((dh // LANES, H * bl, LANES), F32), V((H, ne * nx, bl, dh), BF16),
-                DMA((10,)), DMA((6,)), DMA((6,)), DMA((nm,)), DMA((nm,)), DMA((nx,)), DMA((nx,)),
+                DMA((10,)), DMA((6,)), DMA((6,)), DMA((nm,)), DMA((nm,)), DMA((6,)), DMA((6,)),
                 DMA((nx,)), DMA((nx,)), DMA((40,)), DMA((40,)), DMA((40,)), DMA((40,)), DMA, DMA,
             ],
             compiler_params=pltpu.CompilerParams(collective_id=0, has_side_effects=True,
-                                                 vmem_limit_bytes=60 * 1024 * 1024),
+                                                 vmem_limit_bytes=58 * 1024 * 1024),
         )(lengths, x, Wq, Wk, Wv, Wo, Kc, Vc)
+        n = len(outs)
+        y, kn, vn = pl.pallas_call(
+            _write_out,
+            out_shape=tuple(jax.ShapeDtypeStruct(o.shape, o.dtype) for o in outs),
+            in_specs=[vmem] * n, out_specs=(pl.BlockSpec(memory_space=pl.ANY),) * n, scratch_shapes=[DMA((n,))],
+            compiler_params=pltpu.CompilerParams(vmem_limit_bytes=1024 * 1024),
+        )(*outs)
         return y.reshape(b, d), kn, vn
 
     in_specs = (P('rep', None), P('emb', 'model'), P(), P(), P('model', 'emb'),

time: 73.7 us -> 67.6 us (0.917)
  local copies, waits for them, and re-layouts: 6.17 us -> 0 us
    unnamed x7 -> x0, local copies, waits for them, and re-layouts: 6.17 us -> none
    pallas_call x1 -> x2, Pallas kernels: 66.8 us -> 66.8 us  [the longest x1 64.6 us: local(): pl.pallas_call(functools.partial(_kernel, ne, nm, H), out_shape=(V((ne, n...]
where the time goes in v2:
time: 67.6 us; the launch traced here: 67.5 us
  Pallas kernels  66.8 us (99%)
    pallas_call x1, Pallas kernels, local(): pl.pallas_call(functools.partial(_kernel, ne, nm, H), out_shape=(V((ne, n...  64.6 us
    pallas_call x1, Pallas kernels, local(): pl.pallas_call(_write_out, out_shape=tuple((jax.ShapeDtypeStruct(o.shape,...  2.19 us

profile of v2, /device:TPU:97, one launch (start us, length us, event | category | flops | bytes accessed | tf_op | source)
XLA Modules:
  0.0 67.5 jit_solution(13660163003750948484)
XLA Ops:
  0.6 64.6 %shard_map.103 = (bf16[4,4,2,16,4096]{4,3,2,1,0:T(8,128)(2,1)S(1)}, bf16[512,256]{1,0:T(8,128)(2,1)S(1)}, bf16[512,256]{1,0:T(8,128)(2,1)S(1)}) custom-call(s32[512]{0:T(512)} %lens_ref.1, bf16[512,4096]{1,0:T(8,128)(2,1)} %x_hbm.1, bf16[1024,512]{1,0:T(8,128)(2,1)} %wq_hbm.1, bf16[4096,256]{1,0:T(8,128)(2,1)} %wk_hbm.1, bf16[4096,256]{1,0:T(8,128)(2,1)} %wv_hbm.1, ...), custom_call_target="tpu_custom_call" | custom-call | tf_op jit(solution)/shard_map/pallas_call | solution.py:341
  65.3 2.2 %shard_map.104 = (bf16[4,4,2,16,4096]{4,3,2,1,0:T(8,128)(2,1)}, bf16[512,256]{1,0:T(8,128)(2,1)}, bf16[512,256]{1,0:T(8,128)(2,1)}) custom-call(bf16[4,4,2,16,4096]{4,3,2,1,0:T(8,128)(2,1)S(1)} %get-tuple-element.9.y_in, bf16[512,256]{1,0:T(8,128)(2,1)S(1)} %get-tuple-element.10.kn_in, bf16[512,256]{1,0:T(8,128)(2,1)S(1)} %get-tuple-element.11.vn_in), custom_call_target="tpu_custom_call" | custom-call | tf_op jit(solution)/shard_map/pallas_call | solution.py:360

commit v3 on v2

v3 whole, which is shorter than its diff:
```python
import functools

import jax
import jax.numpy as jnp
from jax import lax
from jax.experimental import pallas as pl
from jax.experimental.pallas import tpu as pltpu
from jax.sharding import PartitionSpec as P

CORES = 2
LANES = 128
GROUPS = 2
F32 = jnp.float32
BF16 = jnp.bfloat16


def _mod(a, n):
    return lax.rem(a + 2 * n, n)


def _kernel(ne, nm, H, lens_ref, x_hbm, wq_hbm, wk_hbm, wv_hbm, wo_hbm, kc_hbm, vc_hbm,
            y_ref, kn_ref, vn_ref,
            xv, wq_v, wkv, k_v, v_v, wo_v, s_opp, s_up, s_dn, s_own, rel_p, rel_m, fin_p, fin_m,
            wo_rel, qb, qr, q32, kv32, o32, o_all,
            lsem, q_ss, q_rs, a_ss, a_rs, w_ss, w_rs, d_ss, d_rs, g_ss, o_rs, y_rs, c_ss, c_rs):
    nx = nm // CORES
    i = lax.axis_index('emb')
    j = lax.axis_index('model')
    X = lax.div(j, CORES)
    c = lax.rem(j, CORES)
    de = xv.shape[2]
    be = s_opp.shape[0]
    bl = qr.shape[2]
    nl = q32.shape[0]
    dh = nl * LANES
    hl = H // nm
    hd, nw = wo_v.shape[1:]
    bg = be // GROUPS
    T = k_v.shape[2]
    scale = dh ** -0.5

    def first(g):
        return pl.multiple_of(i * be + g * bg + j * bl, bl)

    def dev(yy, xx, cc):
        return {'emb': yy, 'model': xx * CORES + cc}

    def row(jj):
        return {'emb': i, 'model': jj}

    def rcopy(src, dst, ss, rs, to):
        return pltpu.make_async_remote_copy(src_ref=src, dst_ref=dst, send_sem=ss, recv_sem=rs,
                                            device_id=to, device_id_type=pl.DeviceIdType.MESH)

    up, dn, opp = _mod(i + 1, ne), _mod(i - 1, ne), _mod(i + 2, ne)
    partner = dev(i, X, 1 - c)

    barrier = pltpu.get_barrier_semaphore()
    for k in range(1, nm):
        pl.semaphore_signal(barrier, inc=1, device_id=row(_mod(j + k, nm)), device_id_type=pl.DeviceIdType.MESH)
    for yy in (up, dn):
        pl.semaphore_signal(barrier, inc=1, device_id={'emb': yy, 'model': j}, device_id_type=pl.DeviceIdType.MESH)

    def load(n, src, dst):
        cp = pltpu.make_async_copy(src, dst, lsem.at[n])
        cp.start()
        return cp

    def xblock(n, blk):
        return load(n, x_hbm.at[:, pl.ds(pl.multiple_of(blk * de, de), de)], xv.at[blk])

    ld_x = [xblock(0, i)]
    ld_wq = load(4, wq_hbm, wq_v)
    ld_x += [xblock(k, _mod(i + k, ne)) for k in range(1, ne)]
    ld_wk = load(5, wk_hbm, wkv.at[:, pl.ds(0, dh)])
    ld_wv = load(6, wv_hbm, wkv.at[:, pl.ds(dh, dh)])
    ld_kv = [(load(8 + 2 * g, kc_hbm.at[pl.ds(first(g), bl)], k_v.at[g]),
              load(9 + 2 * g, vc_hbm.at[pl.ds(first(g), bl)], v_v.at[g])) for g in range(GROUPS)]
    ld_wo = load(7, wo_hbm.at[:, pl.ds(pl.multiple_of(X * nw, nw), nw)], wo_v.at[j])

    sends = []

    def go(cp):
        cp.start()
        sends.append(cp)

    ld_x[0].wait()
    ld_wq.wait()

    def part(d, buf):
        buf[...] = jnp.dot(xv[i, pl.ds(pl.multiple_of(d * be, be), be), :], wq_v[...], preferred_element_type=F32)

    hb = bg // 2
    to_up, to_dn = {'emb': up, 'model': j}, {'emb': dn, 'model': j}

    def lo(g):
        return pl.ds(g * bg, hb)

    def hi(g):
        return pl.ds(g * bg + hb, hb)

    def q_copy(n, g, src, dst, to):
        return rcopy(src, dst, q_ss.at[6 * g + n], q_rs.at[6 * g + n], to)

    def send_opp(g):
        go(q_copy(0, g, s_opp.at[lo(g)], rel_p.at[g], to_up))
        go(q_copy(1, g, s_opp.at[hi(g)], rel_m.at[g], to_dn))

    def send_pure_up(g):
        go(q_copy(2, g, s_up.at[hi(g)], fin_p.at[hi(g)], to_up))

    def send_pure_dn(g):
        go(q_copy(3, g, s_dn.at[lo(g)], fin_m.at[lo(g)], to_dn))

    def relay(g):
        q_copy(0, g, rel_p.at[g], rel_p.at[g], to_up).wait_recv()
        s_up[lo(g), :] = s_up[lo(g), :] + rel_p[g]
        go(q_copy(4, g, s_up.at[lo(g)], fin_p.at[lo(g)], to_up))
        q_copy(1, g, rel_m.at[g], rel_m.at[g], to_dn).wait_recv()
        s_dn[hi(g), :] = s_dn[hi(g), :] + rel_m[g]
        go(q_copy(5, g, s_dn.at[hi(g)], fin_m.at[hi(g)], to_dn))

    def exchange(g):
        for n, ref, to in ((2, fin_p.at[hi(g)], to_up), (3, fin_m.at[lo(g)], to_dn),
                           (4, fin_p.at[lo(g)], to_up), (5, fin_m.at[hi(g)], to_dn)):
            q_copy(n, g, ref, ref, to).wait_recv()
        rows = slice(g * bg, (g + 1) * bg)
        qb[g] = (s_own[rows, :] + fin_p[rows, :] + fin_m[rows, :]).reshape(qb.shape[1:]).astype(BF16)
        for k in range(1, nm):
            t = _mod(j + k, nm)
            go(rcopy(qb.at[g, t], qr.at[g, j], a_ss.at[g * nm + k], a_rs.at[g * nm + k], row(t)))
        qr[g, j] = qb[g, j]

    part(opp, s_opp)
    pl.semaphore_wait(barrier, nm - 1 + 2)
    send_opp(0)
    part(up, s_up)
    send_pure_up(0)
    part(dn, s_dn)
    send_pure_dn(0)
    send_opp(1)

    east, west, far = _mod(X + 1, nx), _mod(X - 1, nx), _mod(X + 2, nx)
    wo_lo, wo_hi = pl.ds(0, hd // 2), pl.ds(hd // 2, hd // 2)

    def wo_cols(rows, t):
        return wo_hbm.at[rows, pl.ds(pl.multiple_of(t * nw, nw), nw)]

    go(rcopy(wo_cols(pl.ds(0, hd), east), wo_v.at[j], w_ss.at[0], w_rs.at[0], dev(i, east, c)))
    go(rcopy(wo_cols(pl.ds(0, hd), west), wo_v.at[j], w_ss.at[1], w_rs.at[1], dev(i, west, c)))
    go(rcopy(wo_cols(wo_lo, far), wo_rel.at[0], w_ss.at[2], w_rs.at[2], dev(i, east, c)))
    go(rcopy(wo_cols(wo_hi, far), wo_rel.at[1], w_ss.at[3], w_rs.at[3], dev(i, west, c)))
    part(i, s_own)

    for ld in ld_x[1:]:
        ld.wait()
    ld_wk.wait()
    ld_wv.wait()

    rows_m = kn_ref.shape[0] // ne

    def kv_rows(m, _):
        rows = pl.ds(pl.multiple_of(m * rows_m, rows_m), rows_m)
        acc = jnp.dot(xv[0, rows, :], wkv[0:de, :], preferred_element_type=F32)
        for blk in range(1, ne):
            acc = acc + jnp.dot(xv[blk, rows, :], wkv[blk * de:(blk + 1) * de, :], preferred_element_type=F32)
        acc = acc.astype(BF16)
        kn_ref[rows, :] = acc[:, :dh]
        vn_ref[rows, :] = acc[:, dh:]
        kv32[rows, :] = acc.astype(F32)
        return 0

    lax.fori_loop(0, ne, kv_rows, 0)

    relay(0)
    send_pure_up(1)
    send_pure_dn(1)
    relay(1)
    exchange(0)
    exchange(1)

    s_west, s_east, s_far = west * CORES + c, east * CORES + c, far * CORES + c
    rcopy(wo_rel.at[0], wo_rel.at[0], w_ss.at[2], w_rs.at[2], partner).wait_recv()
    go(rcopy(wo_rel.at[0], wo_v.at[s_west, wo_lo], w_ss.at[4], w_rs.at[4], dev(i, east, c)))
    rcopy(wo_rel.at[1], wo_rel.at[1], w_ss.at[3], w_rs.at[3], partner).wait_recv()
    go(rcopy(wo_rel.at[1], wo_v.at[s_east, wo_hi], w_ss.at[5], w_rs.at[5], dev(i, west, c)))
    ld_wo.wait()

    def to_core(n, ref):
        go(rcopy(ref, ref, d_ss.at[n], d_rs.at[n], partner))

    def wo_here(n, ref):
        rcopy(ref, ref, w_ss.at[n], w_rs.at[n], partner).wait_recv()
        return ref

    to_core(0, wo_v.at[j])
    to_core(1, wo_here(0, wo_v.at[s_west]))
    to_core(2, wo_here(1, wo_v.at[s_east]))

    chip = i * nx + X

    def attention(g):
        for ld in ld_kv[g]:
            ld.wait()
        for k in range(1, nm):
            src = qr.at[g, _mod(j - k, nm)]
            rcopy(src, src, a_ss.at[g * nm + k], a_rs.at[g * nm + k], partner).wait_recv()
        for jj in range(nm):
            for h in range(hl):
                for n in range(nl):
                    q32[n, (jj * hl + h) * bl:(jj * hl + h + 1) * bl, :] = (
                        qr[g, jj, :, h * dh + n * LANES:h * dh + (n + 1) * LANES].astype(F32))
        new = kv32[pl.ds(first(g), bl), :]
        for b in range(bl):
            q = jnp.concatenate([q32[n, pl.ds(b, H, stride=bl), :] for n in range(nl)], axis=1)
            s = lax.dot_general(q.astype(BF16), k_v[g, b], (((1,), (1,)), ((), ())),
                                preferred_element_type=F32) * scale
            s = jnp.where(lax.broadcasted_iota(jnp.int32, (H, T), 1) < lens_ref[first(g) + b], s, -jnp.inf)
            sn = jnp.sum(q * new[b:b + 1, :dh], axis=1, keepdims=True) * scale
            m = jnp.maximum(jnp.max(s, axis=1, keepdims=True), sn)
            p = jnp.exp(s - m)
            pn = jnp.exp(sn - m)
            l = jnp.sum(p, axis=1, keepdims=True) + pn
            acc = jnp.dot(p.astype(BF16), v_v[g, b], preferred_element_type=F32)
            acc = acc + pn.astype(BF16).astype(F32) * new[b:b + 1, dh:]
            o = acc / l
            for n in range(nl):
                o32[n, pl.ds(b, H, stride=bl), :] = o[:, n * LANES:(n + 1) * LANES]
        for h in range(H):
            for n in range(nl):
                o_all[g, h, chip, :, n * LANES:(n + 1) * LANES] = o32[n, h * bl:(h + 1) * bl, :].astype(BF16)

    class Gather:
        ITEMS = (0, -1, 1, 2)

        def __init__(self, piece, ss, rs, base, arrived):
            self.p, self.ss, self.rs, self.base, self.arrived = piece, ss, rs, base, arrived

        def piece(self, hf, dp, ds, q, n):
            dx, dy = (dp, ds) if hf == 0 else (ds, dp)
            return self.p(_mod(i + dy, ne), _mod(X + dx, nx), 2 * hf + q, n)

        def to(self, hf, dp, ds):
            dx, dy = (dp, ds) if hf == 0 else (ds, dp)
            return dev(_mod(i + dy, ne), _mod(X + dx, nx), c)

        def send(self, hf, mid, ref, to):
            rcopy(ref, ref, self.ss, self.rs.at[self.base + 20 * hf + mid], to).start()

        def wait(self, hf, mid, ref):
            rcopy(ref, ref, self.ss, self.rs.at[self.base + 20 * hf + mid], partner).wait_recv()
            self.arrived(ref)

        def near(self, k):
            for hf in range(2):
                for d, sg in enumerate((1, -1)):
                    self.send(hf, 4 + 2 * k + d, self.piece(hf, self.ITEMS[k], 0, 0, 2), self.to(hf, 0, sg))

        def start(self):
            for hf in range(2):
                for d, sg in enumerate((1, -1)):
                    self.send(hf, d, self.piece(hf, 0, 0, 0, 2), self.to(hf, sg, 0))
            self.near(0)
            self.arrived(self.p(i, X, 0, 4))

        def first(self):
            for hf in range(2):
                for d, sg in enumerate((1, -1)):
                    self.wait(hf, d, self.piece(hf, -sg, 0, 0, 2))
                    self.send(hf, 2 + d, self.piece(hf, -sg, 0, d, 1), self.to(hf, sg, 0))
            self.near(1)
            self.near(2)

        def second(self):
            for hf in range(2):
                for d, sg in enumerate((1, -1)):
                    self.wait(hf, 2 + d, self.piece(hf, 2, 0, d, 1))
            self.near(3)

        def on(self, k):
            for hf in range(2):
                for d, sg in enumerate((1, -1)):
                    self.wait(hf, 4 + 2 * k + d, self.piece(hf, self.ITEMS[k], -sg, 0, 2))
                    self.send(hf, 12 + 2 * k + d, self.piece(hf, self.ITEMS[k], -sg, d, 1), self.to(hf, 0, sg))

        def end(self):
            for k in range(4):
                for hf in range(2):
                    for d, sg in enumerate((1, -1)):
                        self.wait(hf, 12 + 2 * k + d, self.piece(hf, self.ITEMS[k], 2, d, 1))

    hq = H // 4

    def o_gather(g):
        return Gather(lambda yy, xx, q, n: o_all.at[g, pl.ds(q * hq, n * hq), yy * nx + xx],
                      g_ss.at[g], o_rs, 40 * g, lambda ref: None)

    def to_partner(ref):
        rcopy(ref, ref, c_ss, c_rs, partner).start()

    def y_gather(g):
        return Gather(lambda yy, xx, q, n: y_ref.at[pl.ds(q, n), g, :, c, :,
                                                    pl.ds(pl.multiple_of((yy * nx + xx) * nw, nw), nw)],
                      g_ss.at[GROUPS + g], y_rs, 40 * g, to_partner)

    cols = pl.ds(pl.multiple_of(chip * nw, nw), nw)
    mine = pl.ds(pl.multiple_of(X * nw, nw), nw)

    def product(g):
        rows = ne * nx * bl
        acc = None
        for h in range(H):
            t = jnp.dot(o_all[g, h].astype(F32).reshape(rows, dh).astype(BF16),
                        wo_v[h // hl, (h % hl) * dh:(h % hl + 1) * dh, :], preferred_element_type=F32)
            acc = t if acc is None else acc + t
        for r in range(ne):
            for xx in range(nx):
                n = (r * nx + xx) * bl
                res = xv[i, pl.ds(r * be + g * bg + xx * CORES * bl, CORES * bl), mine].astype(F32)
                res = jnp.where(c == 0, res[:bl], res[bl:])
                y_ref[r, g, xx, c, :, cols] = (res + acc[n:n + bl, :].astype(BF16).astype(F32)).astype(BF16)

    o0, o1, y0, y1 = o_gather(0), o_gather(1), y_gather(0), y_gather(1)
    attention(0)
    o0.start()
    attention(1)
    o1.start()
    wo_here(4, wo_v.at[s_far, wo_lo])
    wo_here(5, wo_v.at[s_far, wo_hi])
    to_core(3, wo_v.at[s_far])
    o0.first()
    o0.on(0)
    o0.second()
    o1.first()
    o0.on(1)
    o0.on(2)
    o1.on(0)
    o1.second()
    o0.on(3)
    o1.on(1)
    o1.on(2)
    o0.end()

    for k, src in enumerate((X, west, east, far)):
        ref = wo_v.at[src * CORES + 1 - c]
        rcopy(ref, ref, d_ss.at[k], d_rs.at[k], partner).wait_recv()
    product(0)
    y0.start()
    o1.on(3)
    o1.end()
    product(1)
    y1.start()
    y0.first()
    y0.on(0)
    y0.second()
    y1.first()
    y0.on(1)
    y0.on(2)
    y1.on(0)
    y1.second()
    y0.on(3)
    y1.on(1)
    y1.on(2)
    y0.end()
    y1.on(3)
    y1.end()

    other, own = y_ref.at[:, :, :, 1 - c], y_ref.at[:, :, :, c]
    rcopy(own, other, c_ss, c_rs, partner).wait_recv()
    rcopy(own, other, c_ss, c_rs, partner).wait_send()
    chips = ne * nx - 1
    for g in range(GROUPS):
        ref = o_all.at[g, :, pl.ds(0, chips)]
        rcopy(ref, ref, g_ss.at[g], o_rs.at[0], partner).wait_send()
        ref = y_ref.at[:, g, :, c, :, pl.ds(0, chips * nw)]
        rcopy(ref, ref, g_ss.at[GROUPS + g], y_rs.at[0], partner).wait_send()
    for cp in sends:
        cp.wait_send()


def _write_out(y_in, kn_in, vn_in, y_out, kn_out, vn_out, sem):
    copies = [pltpu.make_async_copy(a, b, sem.at[n])
              for n, (a, b) in enumerate(((y_in, y_out), (kn_in, kn_out), (vn_in, vn_out)))]
    for cp in copies:
        cp.start()
    for cp in copies:
        cp.wait()


def solution(mesh):
    ne = mesh.shape['emb']
    nm = mesh.shape['model']

    def local(x, Wq, Wk, Wv, Wo, Kc, Vc, lengths):
        b, d = x.shape
        de = Wq.shape[0]
        dh = Wk.shape[1]
        hl = Wq.shape[1] // dh
        H = hl * nm
        nx = nm // CORES
        be = b // ne
        bl = be // (nm * GROUPS)
        T = Kc.shape[1]
        nw = Wo.shape[1] // nx
        hd = hl * dh
        V = pltpu.VMEM
        DMA = pltpu.SemaphoreType.DMA
        hbm = pl.BlockSpec(memory_space=pltpu.HBM)
        vmem = pl.BlockSpec(memory_space=pltpu.VMEM)
        outs = pl.pallas_call(
            functools.partial(_kernel, ne, nm, H),
            out_shape=(V((ne, GROUPS, nx, CORES, bl, d), BF16), V((b, dh), BF16), V((b, dh), BF16)),
            in_specs=[pl.BlockSpec(memory_space=pltpu.SMEM)] + [hbm] * 7,
            out_specs=(vmem, vmem, vmem),
            scratch_shapes=[
                V((ne, b, de), BF16), V((de, hd), BF16), V((d, 2 * dh), BF16),
                V((GROUPS, bl, T, dh), BF16), V((GROUPS, bl, T, dh), BF16), V((nm, hd, nw), BF16),
                V((be, hd), F32), V((be, hd), F32), V((be, hd), F32), V((be, hd), F32),
                V((GROUPS, be // GROUPS // 2, hd), F32), V((GROUPS, be // GROUPS // 2, hd), F32),
                V((be, hd), F32), V((be, hd), F32),
                V((2, hd // 2, nw), BF16), V((GROUPS, nm, bl, hd), BF16), V((GROUPS, nm, bl, hd), BF16),
                V((dh // LANES, H * bl, LANES), F32), V((b, 2 * dh), F32),
                V((dh // LANES, H * bl, LANES), F32), V((GROUPS, H, ne * nx, bl, dh), BF16),
                DMA((8 + 2 * GROUPS,)), DMA((6 * GROUPS,)), DMA((6 * GROUPS,)),
                DMA((nm * GROUPS,)), DMA((nm * GROUPS,)), DMA((6,)), DMA((6,)),
                DMA((nx,)), DMA((nx,)), DMA((2 * GROUPS,)), DMA((40 * GROUPS,)), DMA((40 * GROUPS,)), DMA, DMA,
            ],
            compiler_params=pltpu.CompilerParams(collective_id=0, has_side_effects=True,
                                                 vmem_limit_bytes=58 * 1024 * 1024),
        )(lengths, x, Wq, Wk, Wv, Wo, Kc, Vc)
        n = len(outs)
        y, kn, vn = pl.pallas_call(
            _write_out,
            out_shape=tuple(jax.ShapeDtypeStruct(o.shape, o.dtype) for o in outs),
            in_specs=[vmem] * n, out_specs=(pl.BlockSpec(memory_space=pl.ANY),) * n, scratch_shapes=[DMA((n,))],
            compiler_params=pltpu.CompilerParams(vmem_limit_bytes=1024 * 1024),
        )(*outs)
        return y.reshape(b, d), kn, vn

    in_specs = (P('rep', None), P('emb', 'model'), P(), P(), P('model', 'emb'),
                P('rep', None, None), P('rep', None, None), P('rep'))
    out_specs = (P('rep', None), P('rep', None), P('rep', None))
    return jax.shard_map(local, mesh=mesh, in_specs=in_specs, out_specs=out_specs, check_vma=False)
```

time: 67.6 us -> 66.7 us (0.987)
  Pallas kernels: 66.8 us -> 66 us
    pallas_call x1, Pallas kernels: 64.6 us -> 63.8 us  [local(): pl.pallas_call(functools.partial(_kernel, ne, nm, H), out_shape=(V((ne, G...]
where the time goes in v3:
time: 66.7 us; the launch traced here: 66.6 us
  Pallas kernels  66 us (99%)
    pallas_call x1, Pallas kernels, local(): pl.pallas_call(functools.partial(_kernel, ne, nm, H), out_shape=(V((ne, G...  63.8 us
    pallas_call x1, Pallas kernels, local(): pl.pallas_call(_write_out, out_shape=tuple((jax.ShapeDtypeStruct(o.shape,...  2.19 us

profile of v3, /device:TPU:97, one launch (start us, length us, event | category | flops | bytes accessed | tf_op | source)
XLA Modules:
  0.0 66.6 jit_solution(18388442585456849436)
XLA Ops:
  0.6 63.8 %shard_map.103 = (bf16[4,2,4,2,8,4096]{5,4,3,2,1,0:T(8,128)(2,1)S(1)}, bf16[512,256]{1,0:T(8,128)(2,1)S(1)}, bf16[512,256]{1,0:T(8,128)(2,1)S(1)}) custom-call(s32[512]{0:T(512)} %lens_ref.1, bf16[512,4096]{1,0:T(8,128)(2,1)} %x_hbm.1, bf16[1024,512]{1,0:T(8,128)(2,1)} %wq_hbm.1, bf16[4096,256]{1,0:T(8,128)(2,1)} %wk_hbm.1, bf16[4096,256]{1,0:T(8,128)(2,1)} %wv_hbm.1, ...), custom_call_target="tpu_custom_call" | custom-call | tf_op jit(solution)/shard_map/pallas_call | solution.py:410
  64.4 2.2 %shard_map.104 = (bf16[4,2,4,2,8,4096]{5,4,3,2,1,0:T(8,128)(2,1)}, bf16[512,256]{1,0:T(8,128)(2,1)}, bf16[512,256]{1,0:T(8,128)(2,1)}) custom-call(bf16[4,2,4,2,8,4096]{5,4,3,2,1,0:T(8,128)(2,1)S(1)} %get-tuple-element.9.y_in, bf16[512,256]{1,0:T(8,128)(2,1)S(1)} %get-tuple-element.10.kn_in, bf16[512,256]{1,0:T(8,128)(2,1)S(1)} %get-tuple-element.11.vn_in), custom_call_target="tpu_custom_call" | custom-call | tf_op jit(solution)/shard_map/pallas_call | solution.py:432
